TPU v7x, 32 devices: a whole 2x2x4 slice. The times are simulated.
32 devices in a mesh: groups: 2 (over x), hst: 8 (over z, y), head: 2 (over core).
Axes of the slice: x: 2, y: 2, z: 4, core: 2. Of those that a mesh axis runs over, the one named last changes fastest.
Arguments:
- ctx_query: bfloat16 [3072, 64, 128], P(('groups', 'hst'), 'head'), parts along dimension 0, may hold values from -8 to 8
- ctx_key: bfloat16 [3072, 64, 128], P(('groups', 'hst'), 'head'), parts along dimension 0, may hold values from -8 to 8
- ctx_value: bfloat16 [3072, 64, 128], P(('groups', 'hst'), 'head'), parts along dimension 0, may hold values from -6 to 6
- valid: int32 [16], P(('groups', 'hst')), parts along dimension 0, may hold values from 128 to 192
- tail_query: bfloat16 [128, 64, 128], P(('groups', 'hst'), 'head'), parts along dimension 0, may hold values from -8 to 8
- tail_position: int32 [128], P(('groups', 'hst')), parts along dimension 0, may hold values from 1 to 1536
Outputs:
- ctx_out: bfloat16 [3072, 64, 128], P(('groups', 'hst'), 'head'), parts along dimension 0
- tail_out: bfloat16 [128, 64, 128], P(('groups', 'hst'), 'head'), parts along dimension 0
There are 2 independent parts, one for each index of `groups`. A program takes and returns all parts, laid end to end along the dimension named above; each array names one. Nothing has to cross between parts.
All inputs are finite; a program needn't handle non-finite values.
Results may differ from a plain program's by a relative error of at most 0.0043.
Values may be sent and summed in bfloat16 or wider, within the bound.
A program may use at most 128 MiB of HBM per device.

v0:
```python
import math

import jax
import jax.numpy as jnp
from jax import lax
from jax.sharding import PartitionSpec as P

ANCHOR = 128


def broadcast(array, axis, root):
    mine = lax.axis_index(axis) == root
    return lax.psum(jnp.where(mine, array, jnp.zeros_like(array)), axis)


def masked_softmax(scores, mask):
    scores = jnp.where(mask, scores, jnp.float32(-1e30))
    peak = jnp.max(scores, axis=-1)
    weights = jnp.where(mask, jnp.exp(scores - peak[..., None]), jnp.float32(0.0))
    return (peak, weights, jnp.sum(weights, axis=-1))


def local(ctx_query, ctx_key, ctx_value, valid, tail_query, tail_position):
    block, heads, width = ctx_query.shape
    scale = 1.0 / math.sqrt(width)
    host = lax.axis_index("hst")
    anchor_key, anchor_value = (
        broadcast(ctx_key[:ANCHOR], "hst", 0),
        broadcast(ctx_value[:ANCHOR], "hst", 0),
    )
    own_count = valid[0]
    keys = jnp.concatenate([anchor_key, ctx_key], 0)
    values = jnp.concatenate([anchor_value, ctx_value], 0)
    rows = jnp.arange(block)[:, None]
    cols = jnp.arange(block)[None, :]
    own_mask = (cols <= rows) & (cols < own_count)
    anchor_mask = jnp.broadcast_to(host != 0, (block, ANCHOR))
    mask = jnp.concatenate([anchor_mask, own_mask], 1)
    scores = jnp.einsum("qhd,khd->hqk", ctx_query, keys, preferred_element_type=jnp.float32) * scale
    peak, weights, total = masked_softmax(scores, mask[None])
    summed = jnp.einsum(
        "hqk,khd->qhd", weights.astype(jnp.bfloat16), values, preferred_element_type=jnp.float32
    )
    ctx_out = (summed / jnp.transpose(total)[:, :, None]).astype(jnp.bfloat16)
    far_key, far_value, far_query = (
        lax.all_to_all(ctx_key, "hst", split_axis=1, concat_axis=0, tiled=True),
        lax.all_to_all(ctx_value, "hst", split_axis=1, concat_axis=0, tiled=True),
        lax.all_to_all(tail_query, "hst", split_axis=1, concat_axis=0, tiled=True),
    )
    counts, positions = (
        lax.all_gather(valid, "hst", axis=0, tiled=True),
        lax.all_gather(tail_position, "hst", axis=0, tiled=True),
    )
    starts = jnp.cumsum(counts) - counts
    slots = jnp.arange(block)
    key_places = (starts[:, None] + slots[None, :]).reshape(-1)
    live = (slots[None, :] < counts[:, None]).reshape(-1)
    row_mask = live[None, :] & (key_places[None, :] < positions[:, None])
    tail_scores = (
        jnp.einsum("rhd,khd->hrk", far_query, far_key, preferred_element_type=jnp.float32) * scale
    )
    tail_peak, tail_weights, tail_total = masked_softmax(tail_scores, row_mask[None])
    tail_summed = jnp.einsum(
        "hrk,khd->rhd", tail_weights, far_value.astype(jnp.float32), precision=lax.Precision.HIGHEST
    )
    result = (tail_summed / jnp.transpose(tail_total)[:, :, None]).astype(jnp.bfloat16)
    tail_out = lax.all_to_all(result, "hst", split_axis=0, concat_axis=1, tiled=True)
    return (ctx_out, tail_out)


def solution(mesh):
    in_specs = (
        P(("groups", "hst"), "head", None),
        P(("groups", "hst"), "head", None),
        P(("groups", "hst"), "head", None),
        P(("groups", "hst")),
        P(("groups", "hst"), "head", None),
        P(("groups", "hst")),
    )
    out_specs = (P(("groups", "hst"), "head", None), P(("groups", "hst"), "head", None))
    return jax.shard_map(local, mesh=mesh, in_specs=in_specs, out_specs=out_specs, check_vma=False)
```

profile of v0, /device:TPU:28, one launch (start us, length us, event | category | flops | bytes accessed | tf_op | source)
XLA Modules:
  0.0 240.6 jit_solution(3953943348192276413)
XLA Ops:
  7.2 3.3 %copy.20 = bf16[192,32,128]{2,0,1:T(8,128)(2,1)} copy(bf16[192,32,128]{2,1,0:T(8,128)(2,1)} %param.7) | data formatting | bytes 3145728 | tf_op args[1]
  10.5 6.0 %all-to-all-start.1 = ((bf16[192,32,128]{2,0,1:T(8,128)(2,1)}), bf16[192,32,128]{2,0,1:T(8,128)(2,1)S(1)}, u32[]{:S(2)}, u32[]{:S(2)}) async-start(bf16[192,32,128]{2,0,1:T(8,128)(2,1)} %copy.20), calls=%async_computation.1 | async-start | bytes 3145728 | tf_op jit(solution)/shard_map/all_to_all | solution.py:46
  16.5 3.2 %copy.18 = bf16[192,32,128]{2,0,1:T(8,128)(2,1)} copy(bf16[192,32,128]{2,1,0:T(8,128)(2,1)} %param.8) | data formatting | bytes 3145728 | tf_op args[2]
  19.6 2.3 slice_select_fusion.1
  21.9 29.2 %all-to-all-done.1 = bf16[192,32,128]{2,0,1:T(8,128)(2,1)S(1)} async-done(((bf16[192,32,128]{2,0,1:T(8,128)(2,1)}), bf16[192,32,128]{2,0,1:T(8,128)(2,1)S(1)}, u32[]{:S(2)}, u32[]{:S(2)}) %all-to-all-start.1) | async-done | bytes 1572896 | tf_op jit(solution)/shard_map/all_to_all | solution.py:46
  51.1 6.6 %all-to-all-start.2 = ((bf16[192,32,128]{2,0,1:T(8,128)(2,1)}), bf16[192,32,128]{2,0,1:T(8,128)(2,1)}, u32[]{:S(2)}, u32[]{:S(2)}) async-start(bf16[192,32,128]{2,0,1:T(8,128)(2,1)} %copy.18), calls=%async_computation.2 | async-start | bytes 3145728 | tf_op jit(solution)/shard_map/all_to_all | solution.py:47
  57.7 2.3 slice_select_fusion
  60.7 0.6 dynamic-slice
  62.0 0.2 dynamic-update-slice.1
  62.2 0.8 dynamic-update-slice
  63.0 51.7 %all-reduce.3 = (s32[8]{0:T(128)S(1)}, s32[64]{0:T(128)S(1)}) all-reduce(s32[8]{0:T(128)S(1)} %dynamic-update-slice, s32[64]{0:T(128)S(1)} %dynamic-update-slice.1), channel_id=1, replica_groups=mesh['groups'=2,'hst'=8,'head'=2] {'hst'}, use_global_device_ids=true, to_apply=%add.1 | all-reduce | flops 72 | bytes 576
  114.7 0.2 reduce-window.9
  115.0 0.1 lt.55
  115.1 0.1 iota_add_fusion
  115.1 0.1 add.24
  115.2 0.7 copy.23
  115.9 0.1 compare_and_fusion
  116.1 68.5 %all-reduce.7.cloned.1.call-done = (bf16[128,32,128]{2,0,1:T(8,128)(2,1)}, bf16[128,32,128]{2,0,1:T(8,128)(2,1)}) async-done(((bf16[128,32,128]{2,0,1:T(8,128)(2,1)}, bf16[128,32,128]{2,0,1:T(8,128)(2,1)}), (bf16[128,32,128]{2,0,1:T(8,128)(2,1)}, bf16[128,32,128]{2,0,1:T(8,128)(2,1)})) %all-reduce.7.cloned.1.call-update) | async-done | bytes 2097168 | tf_op jit(solution)/shard_map/psum | solution.py:13
  184.6 6.8 %fusion.9 = f32[32,320,192]{1,2,0:T(8,128)} fusion(bf16[192,32,128]{2,0,1:T(8,128)(2,1)} %copy.20, bf16[128,32,128]{2,0,1:T(8,128)(2,1)} %get-tuple-element.8, bf16[192,32,128]{2,1,0:T(8,128)(2,1)S(1)} %copy-done), kind=kOutput, calls=%fused_computation.13 | convolution fusion | flops 508559360 | bytes 12058624 | tf_op jit(solution)/shard_map/qhd,khd->hqk/dot_general | solution.py:39
  191.5 6.1 %all-to-all-start = ((bf16[8,32,128]{2,0,1:T(8,128)(2,1)}), bf16[8,32,128]{2,0,1:T(8,128)(2,1)S(1)}, u32[]{:S(2)}, u32[]{:S(2)}) async-start(bf16[8,32,128]{2,0,1:T(8,128)(2,1)} %copy.23), calls=%async_computation | async-start | bytes 131072 | tf_op jit(solution)/shard_map/all_to_all | solution.py:48
  197.6 14.9 %fusion.37 = (f32[32,192]{1,0:T(8,128)S(1)}, bf16[32,192,320]{2,1,0:T(8,128)(2,1)}) fusion(f32[32,320,192]{1,2,0:T(8,128)} %fusion.9, pred[192,320]{1,0:T(8,128)(4,1)S(1)} %concatenate.10), kind=kOutput, calls=%fused_computation.46 | output fusion | flops 15728959 | bytes 11882496 | tf_op jit(solution)/shard_map/sub | solution.py:19
  212.5 1.3 copy.26
  213.8 2.8 %copy.28 = bf16[192,8,4,128]{3,0,1,2:T(8,128)(2,1)} copy(bf16[192,8,4,128]{3,0,2,1:T(8,128)(2,1)} %bitcast.14) | data formatting | bytes 3145728 | tf_op jit(solution)/shard_map/all_to_all | solution.py:47
  216.6 0.8 fusion.38
  217.3 0.4 fusion.17
  217.8 1.0 copy-done.2
  218.7 1.3 fusion.21
  220.0 0.7 copy.29
  220.7 6.0 %all-to-all-start.3 = ((bf16[64,4,128]{2,1,0:T(4,128)(2,1)}), bf16[64,4,128]{2,1,0:T(4,128)(2,1)S(1)}, u32[]{:S(2)}, u32[]{:S(2)}) async-start(bf16[64,4,128]{2,1,0:T(4,128)(2,1)} %copy.29), calls=%async_computation.3 | async-start | bytes 131072 | tf_op jit(solution)/shard_map/all_to_all | solution.py:67
  226.7 4.2 %fusion.7 = bf16[192,32,128]{2,0,1:T(8,128)(2,1)S(1)} fusion(f32[192,32]{0,1:T(8,128)S(1)} %bitcast.61, bf16[192,32,128]{2,0,1:T(8,128)(2,1)} %copy.18, bf16[128,32,128]{2,0,1:T(8,128)(2,1)S(1)} %copy-done.4, bf16[32,192,320]{2,1,0:T(8,128)(2,1)} %get-tuple-element.11), kind=kOutput, calls=%fused_computation.10 | convolution fusion | flops 510132224 | bytes 8151040 | tf_op jit(solution)/shard_map/hqk,khd->qhd/dot_general | solution.py:41
  231.0 2.2 copy.31
  233.1 0.7 copy.30
  (25 shorter events, 0.2 us)
Async XLA Ops:
  7.2 177.5 %copy-start = (bf16[192,32,128]{2,1,0:T(8,128)(2,1)S(1)}, bf16[192,32,128]{2,1,0:T(8,128)(2,1)}, u32[]{:S(2)}) copy-start(bf16[192,32,128]{2,1,0:T(8,128)(2,1)} %param.6) | copy-start | bytes 4718596
  10.5 40.6 %all-to-all-start.1 = ((bf16[192,32,128]{2,0,1:T(8,128)(2,1)}), bf16[192,32,128]{2,0,1:T(8,128)(2,1)S(1)}, u32[]{:S(2)}, u32[]{:S(2)}) async-start(bf16[192,32,128]{2,0,1:T(8,128)(2,1)} %copy.20), calls=%async_computation.1 | async-start | bytes 3145728 | tf_op jit(solution)/shard_map/all_to_all | solution.py:46
  51.1 140.4 %all-to-all-start.2 = ((bf16[192,32,128]{2,0,1:T(8,128)(2,1)}), bf16[192,32,128]{2,0,1:T(8,128)(2,1)}, u32[]{:S(2)}, u32[]{:S(2)}) async-start(bf16[192,32,128]{2,0,1:T(8,128)(2,1)} %copy.18), calls=%async_computation.2 | async-start | bytes 3145728 | tf_op jit(solution)/shard_map/all_to_all | solution.py:47
  57.7 126.9 %all-reduce.7.cloned.1.call-start = ((), (), s32[]{:S(2)}) async-start(), calls=%async_computation.4 | async-start | bytes 4194304 | tf_op jit(solution)/shard_map/psum | solution.py:13
  60.0 0.7 copy-start.6
  60.0 2.0 copy-start.5
  60.0 55.2 %copy-start.3 = (bf16[8,32,128]{2,1,0:T(8,128)(2,1)S(1)}, bf16[8,32,128]{2,1,0:T(8,128)(2,1)}, u32[]{:S(2)}) copy-start(bf16[8,32,128]{2,1,0:T(8,128)(2,1)} %param.10) | copy-start | bytes 196612
  191.5 25.1 %all-to-all-start = ((bf16[8,32,128]{2,0,1:T(8,128)(2,1)}), bf16[8,32,128]{2,0,1:T(8,128)(2,1)S(1)}, u32[]{:S(2)}, u32[]{:S(2)}) async-start(bf16[8,32,128]{2,0,1:T(8,128)(2,1)} %copy.23), calls=%async_computation | async-start | bytes 131072 | tf_op jit(solution)/shard_map/all_to_all | solution.py:48
  213.8 2.8 %copy-start.1 = (bf16[192,8,4,128]{3,0,1,2:T(8,128)(2,1)S(1)}, bf16[192,8,4,128]{3,0,1,2:T(8,128)(2,1)}, u32[]{:S(2)}) copy-start(bf16[192,8,4,128]{3,0,1,2:T(8,128)(2,1)} %copy.26) | copy-start | bytes 4718596
  217.3 1.4 copy-start.2
  218.7 8.0 %copy-start.4 = (bf16[128,32,128]{2,0,1:T(8,128)(2,1)S(1)}, bf16[128,32,128]{2,0,1:T(8,128)(2,1)}, u32[]{:S(2)}) copy-start(bf16[128,32,128]{2,0,1:T(8,128)(2,1)} %get-tuple-element.9) | copy-start | bytes 3145732
  220.7 12.4 %all-to-all-start.3 = ((bf16[64,4,128]{2,1,0:T(4,128)(2,1)}), bf16[64,4,128]{2,1,0:T(4,128)(2,1)S(1)}, u32[]{:S(2)}, u32[]{:S(2)}) async-start(bf16[64,4,128]{2,1,0:T(4,128)(2,1)} %copy.29), calls=%async_computation.3 | async-start | bytes 131072 | tf_op jit(solution)/shard_map/all_to_all | solution.py:67
Sparse Core Ops, SparseCore 0:
  62.1 122.4 all-reduce.6
where the time goes:
time: 243 us; the launch traced here: 241 us
  waiting for transfers between devices  97.8 us (40%)
  blocking collectives  51.7 us (21%)
  starting transfers between devices  24.7 us (10%)
  other arithmetic  20.4 us (8%)
  local copies, waits for them, and re-layouts  17.5 us (7%)
  between operations  15.4 us (6%)
  matrix products  13.1 us (5%)
    psum x1, waiting for transfers between devices, broadcast(): return lax.psum(jnp.where(mine, array, jnp.zeros_like(array)), axis)  68.5 us
    unnamed x1, blocking collectives  51.7 us
    all_to_all x1, waiting for transfers between devices, local(): lax.all_to_all(ctx_key, 'hst', split_axis=1, concat_axis=0, tiled=True)  29.2 us
    sub x1, other arithmetic, masked_softmax(): scores - peak[..., None]  14.9 us
    unnamed x23, local copies, waits for them, and re-layouts  11.9 us
    dot_general x1, matrix products, local(): jnp.einsum('qhd,khd->hqk', ctx_query, keys, preferred_element_type=jnp.fl...  6.84 us
    all_to_all x1, starting transfers between devices, local(): lax.all_to_all(ctx_value, 'hst', split_axis=1, concat_axis=0, tiled=True)  6.58 us
    all_to_all x1, starting transfers between devices, local(): lax.all_to_all(tail_query, 'hst', split_axis=1, concat_axis=0, tiled=True)  6.13 us
  transfers between devices with their start and end apart: 5, of which 2 were waited for; matrix products, arithmetic and copies ran while one was open for 18% of the time, Pallas kernels for 0%

commit v1 on v0

v1 whole, which is shorter than its diff:
```python
import functools
import math

import jax
import jax.numpy as jnp
from jax import lax
from jax.experimental import pallas as pl
from jax.experimental.pallas import tpu as pltpu
from jax.sharding import PartitionSpec as P

ANCHOR = 128
GROUP = 8
PARTS = 4
NEG = -1e30
MESH = pl.DeviceIdType.MESH


def kernel(
    hosts, block, heads, rows, q_hbm, k_hbm, v_hbm, tq_hbm, info_hbm, out_hbm, tail_ref,
    q_raw, k_raw, v_raw, a_raw, qh, kh, vh, oh, o_raw, qbuf, ibuf, qt, bias, tbias, stat_m, stat_l,
    psend, precv, ssend, srecv, acc,
    load_sem, root_sem, own_sem, out_sem, a_recv, a_send, q_recv, i_recv, q_send, i_send,
    p_recv, s_recv, p_send, s_send,
):
    depth = hosts // 2
    groups = heads // GROUP
    half = groups // 2
    piece_rows = ANCHOR // PARTS
    pieces = half * 2 * PARTS
    per = 2 * PARTS
    total_rows = hosts * rows
    scale = math.log2(math.e) / math.sqrt(q_hbm.shape[-1])
    me = lax.axis_index("hst")
    z, y = me // 2, lax.rem(me, 2)
    root = me == 0

    def remote(src, dst, ssem, rsem, host):
        return pltpu.make_async_remote_copy(
            src_ref=src, dst_ref=dst, send_sem=ssem, recv_sem=rsem,
            device_id={"hst": host}, device_id_type=MESH,
        )

    def loads():
        for i, (hbm, raw) in enumerate(((k_hbm, k_raw), (v_hbm, v_raw), (q_hbm, q_raw))):
            for g in range(groups):
                yield pltpu.make_async_copy(
                    hbm.at[:, pl.ds(g * GROUP, GROUP), :], raw.at[g], load_sem.at[i, g]
                )

    def root_loads():
        for t in range(2):
            for p in range(pieces):
                hbm = k_hbm if (p // PARTS) % 2 == 0 else v_hbm
                g = t * half + p // per
                yield pltpu.make_async_copy(
                    hbm.at[pl.ds((p % PARTS) * piece_rows, piece_rows), pl.ds(g * GROUP, GROUP), :],
                    a_raw.at[t, p], root_sem.at[t, p],
                )

    def own_loads():
        yield pltpu.make_async_copy(tq_hbm, qbuf.at[me], own_sem.at[0])
        yield pltpu.make_async_copy(info_hbm, ibuf.at[me], own_sem.at[1])

    @pl.when(root)
    def _():
        for c in root_loads():
            c.start()

    for c in own_loads():
        c.start()
    for c in loads():
        c.start()

    barrier = pltpu.get_barrier_semaphore()

    def greet(k, _):
        pl.semaphore_signal(
            barrier, inc=1, device_id={"hst": lax.rem(me + k, hosts)}, device_id_type=MESH
        )
        return 0

    lax.fori_loop(1, hosts, greet, 0)
    pl.semaphore_wait(barrier, hosts - 1)

    def q_first(k):
        if k == 0:
            return z * 2 + 1 - y
        return lax.rem(z + k, depth) * 2 + y

    def q_copies(k):
        host = q_first(k)
        return (
            remote(tq_hbm, qbuf.at[me], q_send.at[k], q_recv.at[me], host),
            remote(info_hbm, ibuf.at[me], i_send.at[k], i_recv.at[me], host),
        )

    def q_forward(k):
        slot = lax.rem(z + depth - k, depth) * 2 + y
        host = z * 2 + 1 - y
        return (
            remote(qbuf.at[slot], qbuf.at[slot], q_send.at[depth - 1 + k], q_recv.at[slot], host),
            remote(ibuf.at[slot], ibuf.at[slot], i_send.at[depth - 1 + k], i_recv.at[slot], host),
        )

    def q_wait(slot):
        remote(qbuf.at[slot], qbuf.at[slot], q_send.at[0], q_recv.at[slot], me).wait_recv()
        remote(ibuf.at[slot], ibuf.at[slot], i_send.at[0], i_recv.at[slot], me).wait_recv()

    for k in range(depth):
        for c in q_copies(k):
            c.start()

    def sends(t, p):
        main = 1 - t
        ahead = (y == main) & (z + 1 < depth)
        cross = (y == main) & (z >= 1)
        out = [
            (ahead, a_send.at[t, 0, p], (z + 1) * 2 + main),
            (cross, a_send.at[t, 1, p], z * 2 + 1 - main),
        ]
        if t == 0:
            out.append((root, a_send.at[t, 1, p], 1))
        else:
            out.append(((y == 1) & (z == 1), a_send.at[t, 0, p], 1))
        for cond, sem, host in out:
            yield cond, remote(a_raw.at[t, p], a_raw.at[t, p], sem, a_recv.at[t, p], host)

    def forward(p):
        for t in range(2):
            for cond, copy in sends(t, p):
                @pl.when(cond)
                def _():
                    copy.start()

    def arrive(p):
        @pl.when(jnp.logical_not(root))
        def _():
            for t in range(2):
                remote(
                    a_raw.at[t, p], a_raw.at[t, p], a_send.at[t, 0, p], a_recv.at[t, p], me
                ).wait_recv()
                for cond, copy in sends(t, p):
                    @pl.when(cond)
                    def _():
                        copy.start()

    @pl.when(root)
    def _():
        for c in root_loads():
            c.wait()

        def body(p, _):
            for t in range(2):
                for cond, copy in sends(t, p):
                    @pl.when(cond)
                    def _():
                        copy.start()
            return 0

        lax.fori_loop(0, pieces, body, 0)

    for c in loads():
        c.wait()

    def relayout(g, _):
        at = pl.ds(g * GROUP, GROUP)
        kh[at, pl.ds(ANCHOR, block), :] = jnp.swapaxes(k_raw[g], 0, 1)
        vh[at, pl.ds(ANCHOR, block), :] = jnp.swapaxes(v_raw[g], 0, 1)
        qh[at] = jnp.swapaxes(q_raw[g], 0, 1)
        return 0

    lax.fori_loop(0, groups, relayout, 0)

    for c in own_loads():
        c.wait()
    count = ibuf[me][0:1, 0:1]
    keys = ANCHOR + block
    row = lax.broadcasted_iota(jnp.int32, (block, keys), 0)
    col = lax.broadcasted_iota(jnp.int32, (block, keys), 1)
    slot = col - ANCHOR
    own_bias = jnp.where((slot <= row) & (slot < count), jnp.float32(0.0), jnp.float32(NEG))
    bias[...] = jnp.where(slot < 0, jnp.where(root, jnp.float32(NEG), jnp.float32(0.0)), own_bias)

    for k in range(1, depth):
        q_wait(lax.rem(z + depth - k, depth) * 2 + y)
        for c in q_forward(k):
            c.start()
    for k in range(depth):
        q_wait(k * 2 + 1 - y)

    start = jnp.zeros((1, 1), jnp.int32)
    for s in range(hosts):
        start = start + ibuf[s][0:1, 0:1] * jnp.where(s < me, 1, 0)
    tcol = lax.broadcasted_iota(jnp.int32, (rows, block), 1)
    for s in range(hosts):
        limit = jnp.minimum(ibuf[s][:, 1:2] - start, count)
        tbias[pl.ds(s * rows, rows), :] = jnp.where(tcol < limit, 0.0, NEG).astype(jnp.float32)
    qt[...] = jnp.swapaxes(qbuf[...].reshape(total_rows, heads, -1), 0, 1)

    stat_m[...] = jnp.zeros_like(stat_m)
    stat_l[...] = jnp.zeros_like(stat_l)
    lane = lax.broadcasted_iota(jnp.int32, stat_m.shape, 1)

    def tail_head(h, _):
        own = pl.ds(ANCHOR, block)
        s = lax.dot_general(
            qt[h], kh[h, own, :], (((1,), (1,)), ((), ())), preferred_element_type=jnp.float32
        )
        s = s * scale + tbias[...]
        m = jnp.max(s, axis=-1, keepdims=True)
        w = jnp.exp2(s - m)
        stat_m[...] = jnp.where(lane == h, m, stat_m[...])
        stat_l[...] = jnp.where(lane == h, jnp.sum(w, axis=-1, keepdims=True), stat_l[...])
        high = w.astype(jnp.bfloat16)
        low = (w - high.astype(jnp.float32)).astype(jnp.bfloat16)
        v = vh[h, own, :]
        num = jnp.dot(high, v, preferred_element_type=jnp.float32)
        num = num + jnp.dot(low, v, preferred_element_type=jnp.float32)
        for d in range(hosts):
            psend[d, h] = num[d * rows : (d + 1) * rows].astype(jnp.bfloat16)
        return 0

    def head(h):
        s = lax.dot_general(
            qh[h], kh[h], (((1,), (1,)), ((), ())), preferred_element_type=jnp.float32
        )
        s = s * scale + bias[...]
        m = jnp.max(s, axis=-1, keepdims=True)
        w = jnp.exp2(s - m)
        den = jnp.sum(w, axis=-1, keepdims=True)
        o = jnp.dot(w.astype(jnp.bfloat16), vh[h], preferred_element_type=jnp.float32)
        oh[h] = (o / den).astype(jnp.bfloat16)

    def place(gl):
        for t in range(2):
            at = pl.ds((t * half + gl) * GROUP, GROUP)
            for i, dst in enumerate((kh, vh)):
                raw = a_raw[t, pl.ds(gl * per + i * PARTS, PARTS)]
                dst[at, pl.ds(0, ANCHOR), :] = jnp.swapaxes(
                    raw.reshape(ANCHOR, GROUP, raw.shape[-1]), 0, 1
                )

    def attend(gl, i):
        head((i // GROUP * half + gl) * GROUP + lax.rem(i, GROUP))

    def outs(gl):
        for t in range(2):
            g = t * half + gl
            yield g, pltpu.make_async_copy(
                o_raw.at[g], out_hbm.at[:, pl.ds(g * GROUP, GROUP), :], out_sem.at[g]
            )

    def finish(gl):
        for g, c in outs(gl):
            o_raw[g] = jnp.swapaxes(oh[pl.ds(g * GROUP, GROUP)], 0, 1)
            c.start()

    def p_copies(k):
        host = lax.rem(me + k, hosts)
        return (
            remote(psend.at[host], precv.at[me], p_send.at[k], p_recv.at[me], host),
            remote(ssend.at[host], srecv.at[me], s_send.at[k], s_recv.at[me], host),
        )

    def p_own():
        yield pltpu.make_async_copy(psend.at[me], precv.at[me], own_sem.at[0])
        yield pltpu.make_async_copy(ssend.at[me], srecv.at[me], own_sem.at[1])

    each = heads // per

    def step0(p, _):
        arrive(p)
        lax.fori_loop(0, each, lambda i, c: tail_head(p * each + i, c), 0)
        return 0

    lax.fori_loop(0, per, step0, 0)
    for d in range(hosts):
        ssend[d, 0] = stat_m[pl.ds(d * rows, rows), :]
        ssend[d, 1] = stat_l[pl.ds(d * rows, rows), :]
    place(0)

    for c in p_own():
        c.start()

    def send_part(k, _):
        for c in p_copies(k):
            c.start()
        return 0

    lax.fori_loop(1, hosts, send_part, 0)

    pairs = 2 * GROUP // per
    for gl in range(1, half):
        def step(p, _, gl=gl):
            arrive(gl * per + p)
            for i in range(pairs):
                attend(gl - 1, p * pairs + i)
            return 0

        lax.fori_loop(0, per, step, 0)
        finish(gl - 1)
        place(gl)

    def last(i, _):
        for j in range(2):
            attend(half - 1, i * 2 + j)
        return 0

    lax.fori_loop(0, GROUP, last, 0)
    finish(half - 1)

    for c in p_own():
        c.wait()

    def part_wait(k, _):
        s = lax.rem(me + k, hosts)
        remote(psend.at[s], precv.at[s], p_send.at[k], p_recv.at[s], me).wait_recv()
        remote(ssend.at[s], srecv.at[s], s_send.at[k], s_recv.at[s], me).wait_recv()
        return 0

    lax.fori_loop(1, hosts, part_wait, 0)
    peak = srecv[0, 0]
    for s in range(1, hosts):
        peak = jnp.maximum(peak, srecv[s, 0])
    total = jnp.zeros_like(peak)
    for s in range(hosts):
        total = total + jnp.exp2(srecv[s, 0] - peak) * srecv[s, 1]
    inverse = 1.0 / total
    acc[...] = jnp.zeros_like(acc)

    def merge(s, _):
        w = jnp.exp2(srecv[s, 0] - peak) * inverse
        for h in range(heads):
            acc[h] += w[:, h : h + 1] * precv[s, h].astype(jnp.float32)
        return 0

    lax.fori_loop(0, hosts, merge, 0)
    tail_ref[...] = jnp.swapaxes(acc[...], 0, 1).astype(jnp.bfloat16)

    for k in range(depth):
        for c in q_copies(k):
            c.wait_send()
    for k in range(1, depth):
        for c in q_forward(k):
            c.wait_send()

    def part_sent(k, _):
        for c in p_copies(k):
            c.wait_send()
        return 0

    lax.fori_loop(1, hosts, part_sent, 0)

    def sent(p, _):
        for t in range(2):
            for cond, copy in sends(t, p):
                @pl.when(cond)
                def _():
                    copy.wait_send()
        return 0

    lax.fori_loop(0, pieces, sent, 0)
    for gl in range(half):
        for _, c in outs(gl):
            c.wait()


def local(hosts, ctx_query, ctx_key, ctx_value, valid, tail_query, tail_position):
    block, heads, width = ctx_query.shape
    rows = tail_query.shape[0]
    groups = heads // GROUP
    pieces = groups // 2 * 2 * PARTS
    depth = hosts // 2
    lane = lax.broadcasted_iota(jnp.int32, (rows, 128), 1)
    info = jnp.where(lane == 0, valid[0], tail_position[:, None])
    bf, f32 = jnp.bfloat16, jnp.float32
    dma = pltpu.SemaphoreType.DMA
    anywhere = pl.BlockSpec(memory_space=pl.ANY)
    raw = pltpu.VMEM((groups, block, GROUP, width), bf)
    keys = pltpu.VMEM((heads, ANCHOR + block, width), bf)
    own = pltpu.VMEM((heads, block, width), bf)
    part = pltpu.VMEM((hosts, heads, rows, width), bf)
    stat = pltpu.VMEM((hosts, 2, rows, 128), f32)
    return pl.pallas_call(
        functools.partial(kernel, hosts, block, heads, rows),
        out_shape=(
            jax.ShapeDtypeStruct(ctx_query.shape, bf),
            jax.ShapeDtypeStruct(tail_query.shape, bf),
        ),
        in_specs=[anywhere] * 5,
        out_specs=(anywhere, pl.BlockSpec(memory_space=pltpu.VMEM)),
        scratch_shapes=[
            raw, raw, raw,
            pltpu.VMEM((2, pieces, ANCHOR // PARTS, GROUP, width), bf),
            own, keys, keys, own, raw,
            pltpu.VMEM((hosts, rows, heads, width), bf),
            pltpu.VMEM((hosts, rows, 128), jnp.int32),
            pltpu.VMEM((heads, hosts * rows, width), bf),
            pltpu.VMEM((block, ANCHOR + block), f32),
            pltpu.VMEM((hosts * rows, block), f32),
            pltpu.VMEM((hosts * rows, 128), f32),
            pltpu.VMEM((hosts * rows, 128), f32),
            part, part, stat, stat,
            pltpu.VMEM((heads, rows, width), f32),
            dma((3, groups)), dma((2, pieces)), dma((2,)), dma((groups,)),
            dma((2, pieces)), dma((2, 2, pieces)),
            dma((hosts,)), dma((hosts,)), dma((2 * depth,)), dma((2 * depth,)),
            dma((hosts,)), dma((hosts,)), dma((hosts,)), dma((hosts,)),
        ],
        compiler_params=pltpu.CompilerParams(
            collective_id=0, has_side_effects=True, vmem_limit_bytes=60 * 1024 * 1024
        ),
    )(ctx_query, ctx_key, ctx_value, tail_query, info)


def solution(mesh):
    wide = P(("groups", "hst"), "head", None)
    thin = P(("groups", "hst"))
    return jax.shard_map(
        functools.partial(local, mesh.shape["hst"]), mesh=mesh,
        in_specs=(wide, wide, wide, thin, wide, thin), out_specs=(wide, wide), check_vma=False,
    )
```

time: 243 us -> 289 us (1.19)
  Pallas kernels: 0 us -> 283 us
  waiting for transfers between devices: 97.8 us -> 0 us
  blocking collectives: 51.7 us -> 0 us
  starting transfers between devices: 24.7 us -> 0 us
  other arithmetic: 20.4 us -> 1.32 us
  between operations: 15.4 us -> 1.3 us
  local copies, waits for them, and re-layouts: 17.5 us -> 3.49 us
  matrix products: 13.1 us -> 0 us
    pallas_call x0 -> x1, Pallas kernels: none -> 283 us  [local(): pl.pallas_call(functools.partial(kernel, hosts, block, heads, rows), out_...]
    psum x1 -> x0, waiting for transfers between devices: 68.5 us -> none  [broadcast(): return lax.psum(jnp.where(mine, array, jnp.zeros_like(array)), axis)]
    unnamed x1 -> x0, blocking collectives: 51.7 us -> none
    all_to_all x4 -> x0, waiting for transfers between devices: 29.2 us -> none  [the longest x1 29.2 us: local(): lax.all_to_all(ctx_key, 'hst', split_axis=1, concat_axis=0, tiled=True)]
    all_to_all x4 -> x0, starting transfers between devices: 24.7 us -> none  [the longest x1 6.58 us: local(): lax.all_to_all(ctx_value, 'hst', split_axis=1, concat_axis=0, tiled=True)]
    sub x2 -> x0, other arithmetic: 14.9 us -> none  [the longest x1 14.9 us: masked_softmax(): scores - peak[..., None]]
    dot_general x4 -> x0, matrix products: 13.1 us -> none  [the longest x1 6.84 us: local(): jnp.einsum('qhd,khd->hqk', ctx_query, keys, preferred_element_type=jnp.fl...]
    unnamed x23 -> x4, local copies, waits for them, and re-layouts: 11.9 us -> 3.49 us
  transfers between devices with their start and end apart: 5 -> 0, of which waited for: 2 -> 0; matrix products, arithmetic and copies ran while one was open for 18% -> 0% of each run, Pallas kernels for 0% -> 0%
where the time goes in v1:
time: 289 us
  Pallas kernels  283 us (98%)
  local copies, waits for them, and re-layouts  3.49 us (1%)
    pallas_call x1, Pallas kernels, local(): pl.pallas_call(functools.partial(kernel, hosts, block, heads, rows), out_...  283 us

profile of v1, /device:TPU:28, one launch (start us, length us, event | category | flops | bytes accessed | tf_op | source)
XLA Modules:
  0.0 289.0 jit_solution(3661379151719703550)
XLA Ops:
  1.3 1.3 broadcast_select_fusion.info_hbm
  2.6 282.9 %shard_map.77 = (bf16[192,32,128]{2,1,0:T(8,128)(2,1)}, bf16[8,32,128]{2,1,0:T(8,128)(2,1)}) custom-call(bf16[192,32,128]{2,1,0:T(8,128)(2,1)} %q_hbm.1, bf16[192,32,128]{2,1,0:T(8,128)(2,1)} %k_hbm.1, bf16[192,32,128]{2,1,0:T(8,128)(2,1)} %v_hbm.1, bf16[8,32,128]{2,1,0:T(8,128)(2,1)} %tq_hbm.1, s32[8,128]{1,0:T(8,128)} %broadcast_select_fusion.info_hbm), custom_call_target="tpu_custom_call" | custom-call | tf_op jit(solution)/shard_map/pallas_call | solution.py:384
  285.5 0.0 copy-start
  285.5 2.9 copy.11
  288.3 0.0 copy-done
  288.3 0.6 copy.12
  (1 shorter events, 0.0 us)
Async XLA Ops:
  285.5 2.9 copy-start

commit v2 on v1

--- a/solution.py
+++ b/solution.py
@@ -10,7 +10,9 @@
 
 ANCHOR = 128
 GROUP = 8
-PARTS = 4
+LAG = 3
+FLIGHT = 2
+PARTS = 2
 NEG = -1e30
 MESH = pl.DeviceIdType.MESH
 
@@ -110,95 +112,65 @@
         for c in q_copies(k):
             c.start()
 
-    def sends(t, p):
-        main = 1 - t
-        ahead = (y == main) & (z + 1 < depth)
-        cross = (y == main) & (z >= 1)
-        out = [
-            (ahead, a_send.at[t, 0, p], (z + 1) * 2 + main),
-            (cross, a_send.at[t, 1, p], z * 2 + 1 - main),
-        ]
-        if t == 0:
-            out.append((root, a_send.at[t, 1, p], 1))
-        else:
-            out.append(((y == 1) & (z == 1), a_send.at[t, 0, p], 1))
-        for cond, sem, host in out:
-            yield cond, remote(a_raw.at[t, p], a_raw.at[t, p], sem, a_recv.at[t, p], host)
-
-    def forward(p):
-        for t in range(2):
-            for cond, copy in sends(t, p):
-                @pl.when(cond)
-                def _():
-                    copy.start()
-
-    def arrive(p):
+    def piece(t, p, ssem, host):
+        return remote(a_raw.at[t, p], a_raw.at[t, p], ssem, a_recv.at[t, p], host)
+
+    def main_sends(p):
+        yield z + 1 < depth, piece(1 - y, p, a_send.at[0, p], me + 2)
+        yield z >= 1, piece(1 - y, p, a_send.at[1, p], z * 2 + 1 - y)
+
+    def other_sends(p):
+        yield root, piece(y, p, a_send.at[2, p], 1)
+        yield me == 3, piece(y, p, a_send.at[2, p], 1)
+
+    def go(copies):
+        for cond, copy in copies:
+            @pl.when(cond)
+            def _():
+                copy.start()
+
+    def root_sends(p):
+        return piece(1 - y, p, a_send.at[0, p], me + 2), piece(y, p, a_send.at[2, p], 1)
+
+    def main_step(p):
+        if FLIGHT <= p:
+            @pl.when(root)
+            def _():
+                for done, c in zip(root_sends(p - FLIGHT), root_sends(p)):
+                    done.wait_send()
+                    c.start()
+
         @pl.when(jnp.logical_not(root))
         def _():
-            for t in range(2):
-                remote(
-                    a_raw.at[t, p], a_raw.at[t, p], a_send.at[t, 0, p], a_recv.at[t, p], me
-                ).wait_recv()
-                for cond, copy in sends(t, p):
-                    @pl.when(cond)
-                    def _():
-                        copy.start()
+            piece(1 - y, p, a_send.at[0, p], me).wait_recv()
+            go(main_sends(p))
+
+    def other_step(p, cond):
+        @pl.when(cond)
+        def _():
+            piece(y, p, a_send.at[0, p], me).wait_recv()
+
+            @pl.when(me == 3)
+            def _():
+                piece(y, p, a_send.at[2, p], 1).start()
+
+    def step(p):
+        if p < pieces:
+            main_step(p)
+        if LAG <= p < pieces + LAG:
+            other_step(p - LAG, me > 1)
+        if 2 * LAG <= p < pieces + 2 * LAG:
+            other_step(p - 2 * LAG, me == 1)
 
     @pl.when(root)
     def _():
         for c in root_loads():
             c.wait()
 
-        def body(p, _):
-            for t in range(2):
-                for cond, copy in sends(t, p):
-                    @pl.when(cond)
-                    def _():
-                        copy.start()
-            return 0
-
-        lax.fori_loop(0, pieces, body, 0)
-
-    for c in loads():
-        c.wait()
-
-    def relayout(g, _):
-        at = pl.ds(g * GROUP, GROUP)
-        kh[at, pl.ds(ANCHOR, block), :] = jnp.swapaxes(k_raw[g], 0, 1)
-        vh[at, pl.ds(ANCHOR, block), :] = jnp.swapaxes(v_raw[g], 0, 1)
-        qh[at] = jnp.swapaxes(q_raw[g], 0, 1)
-        return 0
-
-    lax.fori_loop(0, groups, relayout, 0)
-
-    for c in own_loads():
-        c.wait()
-    count = ibuf[me][0:1, 0:1]
-    keys = ANCHOR + block
-    row = lax.broadcasted_iota(jnp.int32, (block, keys), 0)
-    col = lax.broadcasted_iota(jnp.int32, (block, keys), 1)
-    slot = col - ANCHOR
-    own_bias = jnp.where((slot <= row) & (slot < count), jnp.float32(0.0), jnp.float32(NEG))
-    bias[...] = jnp.where(slot < 0, jnp.where(root, jnp.float32(NEG), jnp.float32(0.0)), own_bias)
-
-    for k in range(1, depth):
-        q_wait(lax.rem(z + depth - k, depth) * 2 + y)
-        for c in q_forward(k):
-            c.start()
-    for k in range(depth):
-        q_wait(k * 2 + 1 - y)
-
-    start = jnp.zeros((1, 1), jnp.int32)
-    for s in range(hosts):
-        start = start + ibuf[s][0:1, 0:1] * jnp.where(s < me, 1, 0)
-    tcol = lax.broadcasted_iota(jnp.int32, (rows, block), 1)
-    for s in range(hosts):
-        limit = jnp.minimum(ibuf[s][:, 1:2] - start, count)
-        tbias[pl.ds(s * rows, rows), :] = jnp.where(tcol < limit, 0.0, NEG).astype(jnp.float32)
-    qt[...] = jnp.swapaxes(qbuf[...].reshape(total_rows, heads, -1), 0, 1)
-
-    stat_m[...] = jnp.zeros_like(stat_m)
-    stat_l[...] = jnp.zeros_like(stat_l)
+        for p in range(FLIGHT):
+            for c in root_sends(p):
+                c.start()
+
     lane = lax.broadcasted_iota(jnp.int32, stat_m.shape, 1)
 
     def tail_head(h, _):
@@ -266,48 +238,107 @@
         yield pltpu.make_async_copy(psend.at[me], precv.at[me], own_sem.at[0])
         yield pltpu.make_async_copy(ssend.at[me], srecv.at[me], own_sem.at[1])
 
-    each = heads // per
-
-    def step0(p, _):
-        arrive(p)
-        lax.fori_loop(0, each, lambda i, c: tail_head(p * each + i, c), 0)
-        return 0
-
-    lax.fori_loop(0, per, step0, 0)
-    for d in range(hosts):
-        ssend[d, 0] = stat_m[pl.ds(d * rows, rows), :]
-        ssend[d, 1] = stat_l[pl.ds(d * rows, rows), :]
-    place(0)
-
-    for c in p_own():
-        c.start()
+    def load_wait(lo, hi):
+        for i, c in enumerate(loads()):
+            if lo * groups <= i < hi * groups:
+                c.wait()
+
+    def keys_item():
+        load_wait(0, 2)
+
+        def body(g, _):
+            at = pl.ds(g * GROUP, GROUP)
+            kh[at, pl.ds(ANCHOR, block), :] = jnp.swapaxes(k_raw[g], 0, 1)
+            vh[at, pl.ds(ANCHOR, block), :] = jnp.swapaxes(v_raw[g], 0, 1)
+            return 0
+
+        lax.fori_loop(0, groups, body, 0)
+
+    def query_item():
+        load_wait(2, 3)
+
+        def body(g, _):
+            qh[pl.ds(g * GROUP, GROUP)] = jnp.swapaxes(q_raw[g], 0, 1)
+            return 0
+
+        lax.fori_loop(0, groups, body, 0)
+
+    def bias_item():
+        for c in own_loads():
+            c.wait()
+        count = ibuf[me][0:1, 0:1]
+        keys = ANCHOR + block
+        row = lax.broadcasted_iota(jnp.int32, (block, keys), 0)
+        col = lax.broadcasted_iota(jnp.int32, (block, keys), 1)
+        slot = col - ANCHOR
+        own_bias = jnp.where((slot <= row) & (slot < count), jnp.float32(0.0), jnp.float32(NEG))
+        bias[...] = jnp.where(slot < 0, jnp.where(root, jnp.float32(NEG), jnp.float32(0.0)), own_bias)
+        stat_m[...] = jnp.zeros_like(stat_m)
+        stat_l[...] = jnp.zeros_like(stat_l)
+
+    def rows_item():
+        for k in range(1, depth):
+            q_wait(lax.rem(z + depth - k, depth) * 2 + y)
+            for c in q_forward(k):
+                c.start()
+
+    def rows_done_item():
+        count = ibuf[me][0:1, 0:1]
+        for k in range(depth):
+            q_wait(k * 2 + 1 - y)
+
+        start = jnp.zeros((1, 1), jnp.int32)
+        for s in range(hosts):
+            start = start + ibuf[s][0:1, 0:1] * jnp.where(s < me, 1, 0)
+        tcol = lax.broadcasted_iota(jnp.int32, (rows, block), 1)
+        for s in range(hosts):
+            limit = jnp.minimum(ibuf[s][:, 1:2] - start, count)
+            tbias[pl.ds(s * rows, rows), :] = jnp.where(tcol < limit, 0.0, NEG).astype(jnp.float32)
+        qt[...] = jnp.swapaxes(qbuf[...].reshape(total_rows, heads, -1), 0, 1)
+
+    def tail_item(i):
+        lax.fori_loop(i * 4, min(i * 4 + 4, heads), tail_head, 0)
+
+    def send_item():
+        for d in range(hosts):
+            ssend[d, 0] = stat_m[pl.ds(d * rows, rows), :]
+            ssend[d, 1] = stat_l[pl.ds(d * rows, rows), :]
+        for c in p_own():
+            c.start()
+        lax.fori_loop(1, hosts, send_part, 0)
+
+    def attend_item(gl, i):
+        def body(j, _):
+            for k in range(2):
+                attend(gl, i * 4 + j * 2 + k)
+            return 0
+
+        lax.fori_loop(0, 2, body, 0)
 
     def send_part(k, _):
         for c in p_copies(k):
             c.start()
         return 0
 
-    lax.fori_loop(1, hosts, send_part, 0)
-
-    pairs = 2 * GROUP // per
-    for gl in range(1, half):
-        def step(p, _, gl=gl):
-            arrive(gl * per + p)
-            for i in range(pairs):
-                attend(gl - 1, p * pairs + i)
-            return 0
-
-        lax.fori_loop(0, per, step, 0)
-        finish(gl - 1)
+    work = [keys_item, rows_item, bias_item, rows_done_item, query_item]
+    work += [functools.partial(tail_item, i) for i in range(heads // 4)]
+    work += [send_item]
+    at = 0
+    for item in work:
+        step(at)
+        at += 1
+        item()
+    for gl in range(half):
+        need = (gl + 1) * per + 2 * LAG
+        while at < need:
+            step(at)
+            at += 1
         place(gl)
-
-    def last(i, _):
-        for j in range(2):
-            attend(half - 1, i * 2 + j)
-        return 0
-
-    lax.fori_loop(0, GROUP, last, 0)
-    finish(half - 1)
+        for i in range(2 * GROUP // 4):
+            step(at)
+            at += 1
+            attend_item(gl, i)
+        finish(gl)
 
     for c in p_own():
         c.wait()
@@ -352,11 +383,10 @@
     lax.fori_loop(1, hosts, part_sent, 0)
 
     def sent(p, _):
-        for t in range(2):
-            for cond, copy in sends(t, p):
-                @pl.when(cond)
-                def _():
-                    copy.wait_send()
+        for cond, copy in (*main_sends(p), *other_sends(p)):
+            @pl.when(cond & (jnp.logical_not(root) | (p >= pieces - FLIGHT)))
+            def _():
+                copy.wait_send()
         return 0
 
     lax.fori_loop(0, pieces, sent, 0)
@@ -403,7 +433,7 @@
             part, part, stat, stat,
             pltpu.VMEM((heads, rows, width), f32),
             dma((3, groups)), dma((2, pieces)), dma((2,)), dma((groups,)),
-            dma((2, pieces)), dma((2, 2, pieces)),
+            dma((2, pieces)), dma((3, pieces)),
             dma((hosts,)), dma((hosts,)), dma((2 * depth,)), dma((2 * depth,)),
             dma((hosts,)), dma((hosts,)), dma((hosts,)), dma((hosts,)),
         ],

time: 289 us -> 79.2 us (0.27)
  Pallas kernels: 283 us -> 72.9 us
    pallas_call x1, Pallas kernels: 283 us -> 72.9 us  [local(): pl.pallas_call(functools.partial(kernel, hosts, block, heads, rows), out_...]
where the time goes in v2:
time: 79.2 us; the launch traced here: 79 us
  Pallas kernels  72.9 us (92%)
  local copies, waits for them, and re-layouts  3.49 us (4%)
  other arithmetic  1.32 us (2%)
  between operations  1.3 us (2%)
    pallas_call x1, Pallas kernels, local(): pl.pallas_call(functools.partial(kernel, hosts, block, heads, rows), out_...  72.9 us
    unnamed x4, local copies, waits for them, and re-layouts  3.49 us

profile of v2, /device:TPU:28, one launch (start us, length us, event | category | flops | bytes accessed | tf_op | source)
XLA Modules:
  0.0 79.0 jit_solution(1201591098010524695)
XLA Ops:
  1.3 1.3 %broadcast_select_fusion.info_hbm = s32[8,128]{1,0:T(8,128)} fusion(s32[8]{0:T(128)} %param.11, s32[]{:T(128)} %bitcast.1, pred[128]{0:T(512)(128)(4,1)S(1)} %iota_compare_fusion), kind=kLoop, calls=%fused_computation | loop fusion | flops 1024 | bytes 4260 | tf_op jit(solution)/shard_map/jit(_where)/select_n | solution.py:405
  2.6 72.9 %shard_map.77 = (bf16[192,32,128]{2,1,0:T(8,128)(2,1)}, bf16[8,32,128]{2,1,0:T(8,128)(2,1)}) custom-call(bf16[192,32,128]{2,1,0:T(8,128)(2,1)} %q_hbm.1, bf16[192,32,128]{2,1,0:T(8,128)(2,1)} %k_hbm.1, bf16[192,32,128]{2,1,0:T(8,128)(2,1)} %v_hbm.1, bf16[8,32,128]{2,1,0:T(8,128)(2,1)} %tq_hbm.1, s32[8,128]{1,0:T(8,128)} %broadcast_select_fusion.info_hbm), custom_call_target="tpu_custom_call" | custom-call | tf_op jit(solution)/shard_map/pallas_call | solution.py:414
  75.5 0.0 copy-start
  75.5 2.9 %copy.11 = bf16[192,32,128]{2,1,0:T(8,128)(2,1)} copy(bf16[192,32,128]{2,1,0:T(8,128)(2,1)} %get-tuple-element.4) | data formatting | bytes 3145728
  78.4 0.0 copy-done
  78.4 0.6 copy.12
  (1 shorter events, 0.0 us)
Async XLA Ops:
  75.5 2.9 %copy-start = (bf16[8,32,128]{2,1,0:T(8,128)(2,1)S(1)}, bf16[8,32,128]{2,1,0:T(8,128)(2,1)}, u32[]{:S(2)}) copy-start(bf16[8,32,128]{2,1,0:T(8,128)(2,1)} %get-tuple-element.5) | copy-start | bytes 196612

commit v3 on v2

--- a/solution.py
+++ b/solution.py
@@ -297,7 +297,7 @@
         qt[...] = jnp.swapaxes(qbuf[...].reshape(total_rows, heads, -1), 0, 1)
 
     def tail_item(i):
-        lax.fori_loop(i * 4, min(i * 4 + 4, heads), tail_head, 0)
+        lax.fori_loop(i * 4, min(i * 4 + 4, heads), tail_head, 0, unroll=2)
 
     def send_item():
         for d in range(hosts):
@@ -309,11 +309,11 @@
 
     def attend_item(gl, i):
         def body(j, _):
-            for k in range(2):
-                attend(gl, i * 4 + j * 2 + k)
+            for k in range(4):
+                attend(gl, i * 4 + j * 4 + k)
             return 0
 
-        lax.fori_loop(0, 2, body, 0)
+        lax.fori_loop(0, 1, body, 0)
 
     def send_part(k, _):
         for c in p_copies(k):

time: 79.2 us -> 78 us (0.985)
  Pallas kernels: 72.9 us -> 71.7 us
    pallas_call x1, Pallas kernels: 72.9 us -> 71.7 us  [local(): pl.pallas_call(functools.partial(kernel, hosts, block, heads, rows), out_...]
where the time goes in v3:
time: 78 us; the launch traced here: 77.8 us
  Pallas kernels  71.7 us (92%)
  local copies, waits for them, and re-layouts  3.49 us (4%)
  other arithmetic  1.32 us (2%)
  between operations  1.3 us (2%)
    pallas_call x1, Pallas kernels, local(): pl.pallas_call(functools.partial(kernel, hosts, block, heads, rows), out_...  71.7 us
    unnamed x4, local copies, waits for them, and re-layouts  3.49 us

profile of v3, /device:TPU:28, one launch (start us, length us, event | category | flops | bytes accessed | tf_op | source)
XLA Modules:
  0.0 77.8 jit_solution(13074342447333163974)
XLA Ops:
  1.3 1.3 %broadcast_select_fusion.info_hbm = s32[8,128]{1,0:T(8,128)} fusion(s32[8]{0:T(128)} %param.11, s32[]{:T(128)} %bitcast.1, pred[128]{0:T(512)(128)(4,1)S(1)} %iota_compare_fusion), kind=kLoop, calls=%fused_computation | loop fusion | flops 1024 | bytes 4260 | tf_op jit(solution)/shard_map/jit(_where)/select_n | solution.py:405
  2.6 71.7 %shard_map.77 = (bf16[192,32,128]{2,1,0:T(8,128)(2,1)}, bf16[8,32,128]{2,1,0:T(8,128)(2,1)}) custom-call(bf16[192,32,128]{2,1,0:T(8,128)(2,1)} %q_hbm.1, bf16[192,32,128]{2,1,0:T(8,128)(2,1)} %k_hbm.1, bf16[192,32,128]{2,1,0:T(8,128)(2,1)} %v_hbm.1, bf16[8,32,128]{2,1,0:T(8,128)(2,1)} %tq_hbm.1, s32[8,128]{1,0:T(8,128)} %broadcast_select_fusion.info_hbm), custom_call_target="tpu_custom_call" | custom-call | tf_op jit(solution)/shard_map/pallas_call | solution.py:414
  74.4 0.0 copy-start
  74.4 2.9 %copy.11 = bf16[192,32,128]{2,1,0:T(8,128)(2,1)} copy(bf16[192,32,128]{2,1,0:T(8,128)(2,1)} %get-tuple-element.4) | data formatting | bytes 3145728
  77.2 0.0 copy-done
  77.2 0.6 copy.12
  (1 shorter events, 0.0 us)
Async XLA Ops:
  74.4 2.9 %copy-start = (bf16[8,32,128]{2,1,0:T(8,128)(2,1)S(1)}, bf16[8,32,128]{2,1,0:T(8,128)(2,1)}, u32[]{:S(2)}) copy-start(bf16[8,32,128]{2,1,0:T(8,128)(2,1)} %get-tuple-element.5) | copy-start | bytes 196612
